TPU v7x, 32 devices: a whole 2x2x4 slice. The times are simulated.
32 devices in a mesh: seq: 8 (over z, x), feat: 4 (over y, core).
Axes of the slice: x: 2, y: 2, z: 4, core: 2. Of those that a mesh axis runs over, the one named last changes fastest.
Arguments:
- injection: bfloat16 [1024, 5120], P('seq', 'feat'), may hold values from -8 to 8
- warm_start: bfloat16 [1024, 5120], P('seq', 'feat'), may hold values from -12 to 12
- gain_in: float32 [5120], replicated, may hold values from 0.5 to 1.5
- gain_out: float32 [5120], replicated, may hold values from 0.5 to 1.5
- w_query: bfloat16 [5120, 5120], P(None, 'feat'), may hold values from -0.0848993624 to 0.0848993624
- w_key: bfloat16 [5120, 1024], P(None, 'feat'), may hold values from -0.0848993624 to 0.0848993624
- w_value: bfloat16 [5120, 1024], P(None, 'feat'), may hold values from -0.078125 to 0.078125
- w_out: bfloat16 [5120, 5120], P('feat'), may hold values from -0.078125 to 0.078125
Outputs:
- equilibrium: float32 [1024, 5120], P('seq', 'feat')
All inputs are finite; a program needn't handle non-finite values.
Results may differ from a plain program's by a relative error of at most 0.009.
Values may be sent and summed in bfloat16 or wider, within the bound.
A program may use at most 128 MiB of HBM per device.

v0:
```python
import math

import jax
import jax.numpy as jnp
from jax import lax
from jax.sharding import PartitionSpec as P

HEADS = 40
KV_HEADS = 8
HEAD_DIM = 128
ITERS = 4


EPS = 1e-06
LAMBDA = 0.03


def solve_small(matrix, target):
    size_now = target.shape[0]
    row_list = [matrix[idx_row] for idx_row in range(size_now)]
    value_list = [target[idx_row] for idx_row in range(size_now)]
    for pivot_at in range(size_now):
        for below_at in range(pivot_at + 1, size_now):
            ratio_now = row_list[below_at][pivot_at] / row_list[pivot_at][pivot_at]
            row_list[below_at] = row_list[below_at] - ratio_now * row_list[pivot_at]
            value_list[below_at] = value_list[below_at] - ratio_now * value_list[pivot_at]
    result_list = [None] * size_now
    for pivot_at in reversed(range(size_now)):
        running = value_list[pivot_at]
        for later_at in range(pivot_at + 1, size_now):
            running = running - row_list[pivot_at][later_at] * result_list[later_at]
        result_list[pivot_at] = running / row_list[pivot_at][pivot_at]
    return jnp.stack(result_list)


def coefficients(gram_matrix, scale_all):
    history_len = gram_matrix.shape[0]
    system = gram_matrix / scale_all + LAMBDA * jnp.eye(history_len, dtype=jnp.float32)
    unscaled = solve_small(system, jnp.ones((history_len,), jnp.float32))
    return unscaled / jnp.sum(unscaled)


def on_device(injection, warm_start, gain_in, gain_out, w_query, w_key, w_value, w_out):
    seq_at = lax.axis_index("seq")
    tok_dev = injection.shape[0]
    width = gain_in.shape[0]
    head_cols = w_query.shape[1]
    kv_cols = w_key.shape[1]
    kv_local = kv_cols // HEAD_DIM
    group = HEADS // KV_HEADS
    scale_all = float(tok_dev * lax.axis_size("seq") * width)
    score_scale = 1.0 / math.sqrt(HEAD_DIM)
    w_joined = jnp.concatenate([w_query, w_key, w_value], axis=1)
    query_pos = seq_at * tok_dev + jnp.arange(tok_dev, dtype=jnp.int32)
    injection_here, start_here = (
        lax.all_to_all(injection, "feat", split_axis=0, concat_axis=1, tiled=True),
        lax.all_to_all(warm_start, "feat", split_axis=0, concat_axis=1, tiled=True),
    )
    injection_full = injection_here.astype(jnp.float32)
    current = start_here.astype(jnp.float32)
    evaluated = []
    residuals = []
    for iteration in range(ITERS):
        mixed = current + injection_full
        normed = (
            mixed * lax.rsqrt(jnp.mean(mixed * mixed, axis=1, keepdims=True) + EPS) * gain_in
        ).astype(jnp.bfloat16)
        layer_joined = jnp.dot(
            lax.all_gather(normed, "feat", axis=0, tiled=True),
            w_joined,
            preferred_element_type=jnp.float32,
        ).astype(jnp.bfloat16)
        queries = layer_joined[:, :head_cols].reshape(tok_dev, kv_local, group, HEAD_DIM)
        key_rows = layer_joined[:, head_cols : head_cols + kv_cols]
        value_rows = layer_joined[:, head_cols + kv_cols :]
        start_max = jnp.full((tok_dev, kv_local, group), -1e30, jnp.float32)
        run_max = start_max
        key_piece = lax.all_gather(key_rows, "seq", axis=0, tiled=True)
        value_piece = lax.all_gather(value_rows, "seq", axis=0, tiled=True)
        length = key_piece.shape[0]
        key_heads = key_piece.reshape(length, kv_local, HEAD_DIM)
        value_heads = value_piece.reshape(length, kv_local, HEAD_DIM)
        scores = (
            jnp.einsum("tkgd,skd->tkgs", queries, key_heads, preferred_element_type=jnp.float32)
            * score_scale
        )
        key_pos = jnp.arange(length, dtype=jnp.int32)
        allowed = (query_pos[:, None] >= key_pos[None, :])[:, None, None, :]
        scores = jnp.where(allowed, scores, -1e30)
        new_max = jnp.maximum(run_max, jnp.max(scores, axis=3))
        weights = jnp.where(allowed, jnp.exp(scores - new_max[..., None]), 0.0)
        run_sum = jnp.sum(weights, axis=3)
        run_acc = jnp.einsum(
            "tkgs,skd->tkgd",
            weights.astype(jnp.bfloat16),
            value_heads,
            preferred_element_type=jnp.float32,
        )
        run_max, run_sum, run_acc = (new_max, run_sum, run_acc)
        attended = (run_acc / run_sum[..., None]).astype(jnp.bfloat16).reshape(tok_dev, head_cols)
        update = lax.psum_scatter(
            jnp.dot(attended, w_out, preferred_element_type=jnp.float32),
            "feat",
            scatter_dimension=0,
            tiled=True,
        )
        summed = mixed + update
        image = (
            summed * lax.rsqrt(jnp.mean(summed * summed, axis=1, keepdims=True) + EPS) * gain_out
        )
        evaluated.append(image)
        residuals.append(image - current)
        if iteration == 0:
            current = image
        else:
            history_len = iteration + 1
            stacked = jnp.stack(residuals).reshape(history_len, -1)
            local_gram = jnp.dot(stacked, stacked.T, precision=lax.Precision.HIGHEST)
            gram_matrix = lax.psum(local_gram, ("seq", "feat"))
            weights_now = coefficients(gram_matrix, scale_all)
            current = weights_now[0] * evaluated[0]
            for other in range(1, history_len):
                current = current + weights_now[other] * evaluated[other]
    return lax.all_to_all(current, "feat", split_axis=1, concat_axis=0, tiled=True)


def solution(mesh):
    in_specs = (
        P("seq", "feat"),
        P("seq", "feat"),
        P(),
        P(),
        P(None, "feat"),
        P(None, "feat"),
        P(None, "feat"),
        P("feat", None),
    )
    out_specs = P("seq", "feat")
    return jax.shard_map(
        on_device, mesh=mesh, in_specs=in_specs, out_specs=out_specs, check_vma=False
    )
```

profile of v0, /device:TPU:0, one launch (start us, length us, event | category | flops | bytes accessed | tf_op | source)
XLA Modules:
  0.0 838.7 jit_solution(10279321022507677067)
XLA Ops:
  6.5 11.1 %all_to_all.45 = bf16[4,32,1280]{2,1,0:T(8,128)(2,1)S(1)} all-to-all(bf16[4,32,1280]{2,1,0:T(8,128)(2,1)} %bitcast.259), channel_id=1, replica_groups=mesh['seq'=8,'feat'=4] {'feat'}, dimensions={0} | all-to-all | bytes 655360 | tf_op jit(solution)/shard_map/all_to_all | solution.py:56
  29.1 10.9 %constant_dynamic-update-slice_fusion.2 = bf16[5120,1792]{1,0:T(8,128)(2,1)} fusion(bf16[5120,1280]{1,0:T(8,128)(2,1)} %param.12), kind=kLoop, calls=%fused_computation.95 | loop fusion | bytes 26214400
  58.2 31.4 %all_gather.37 = bf16[1024,256]{1,0:T(8,128)(2,1)S(1)} all-gather(bf16[128,256]{1,0:T(8,128)(2,1)S(1)} %get-tuple-element.30), channel_id=1, replica_groups=mesh['seq'=8,'feat'=4] {'seq'}, dimensions={0}, use_global_device_ids=true | all-gather | bytes 589824 | tf_op jit(solution)/shard_map/all_gather | solution.py:79
  92.6 33.4 %all_gather.38 = bf16[1024,256]{1,0:T(8,128)(2,1)} all-gather(bf16[128,256]{1,0:T(8,128)(2,1)S(1)} %get-tuple-element.29), channel_id=1, replica_groups=mesh['seq'=8,'feat'=4] {'seq'}, dimensions={0}, use_global_device_ids=true | all-gather | bytes 589824 | tf_op jit(solution)/shard_map/all_gather | solution.py:78
  136.5 34.7 %reduce-scatter.5.cloned.1.call-done = f32[32,5120]{1,0:T(8,128)} async-done(((f32[128,5120]{1,0:T(8,128)}), f32[32,5120]{1,0:T(8,128)}) %reduce-scatter.5.cloned.1.call-update) | async-done | bytes 655376 | tf_op jit(solution)/shard_map/reduce_scatter | solution.py:101
  174.9 18.0 %all-gather.7.cloned.1.call-done = bf16[128,5120]{1,0:T(8,128)(2,1)} async-done(((bf16[32,5120]{1,0:T(8,128)(2,1)}), bf16[128,5120]{1,0:T(8,128)(2,1)}) %all-gather.7.cloned.1.call-update) | async-done | bytes 1310736 | tf_op jit(solution)/shard_map/all_gather | solution.py:69
  202.8 31.4 %all_gather.40 = bf16[1024,256]{1,0:T(8,128)(2,1)S(1)} all-gather(bf16[128,256]{1,0:T(8,128)(2,1)S(1)} %get-tuple-element.28), channel_id=1, replica_groups=mesh['seq'=8,'feat'=4] {'seq'}, dimensions={0}, use_global_device_ids=true | all-gather | bytes 589824 | tf_op jit(solution)/shard_map/all_gather | solution.py:79
  237.2 33.4 %all_gather.41 = bf16[1024,256]{1,0:T(8,128)(2,1)} all-gather(bf16[128,256]{1,0:T(8,128)(2,1)S(1)} %get-tuple-element.27), channel_id=1, replica_groups=mesh['seq'=8,'feat'=4] {'seq'}, dimensions={0}, use_global_device_ids=true | all-gather | bytes 589824 | tf_op jit(solution)/shard_map/all_gather | solution.py:78
  281.5 34.2 %reduce-scatter.7.cloned.1.call-done = f32[32,5120]{1,0:T(8,128)} async-done(((f32[128,5120]{1,0:T(8,128)}), f32[32,5120]{1,0:T(8,128)}) %reduce-scatter.7.cloned.1.call-update) | async-done | bytes 655376 | tf_op jit(solution)/shard_map/reduce_scatter | solution.py:101
  319.5 12.0 %fusion.48 = f32[2,2]{1,0:T(2,128)S(1)} fusion(f32[2,32,5120]{2,1,0:T(8,128)S(1)} %pad_maximum_fusion.2), kind=kOutput, calls=%fused_computation.47 | convolution fusion | flops 7864320 | bytes 1310736 | tf_op jit(solution)/shard_map/dot_general | solution.py:118
  331.5 39.2 %psum.21 = f32[2,2]{1,0:T(2,128)S(1)} all-reduce(f32[2,2]{1,0:T(2,128)S(1)} %fusion.48), channel_id=1, replica_groups=mesh['seq'=8,'feat'=4] {'seq','feat'}, use_global_device_ids=true, to_apply=%region_10.11 | all-reduce | flops 4 | bytes 32 | tf_op jit(solution)/shard_map/psum | solution.py:119
  379.4 18.8 %all-gather.9.cloned.1.call-done = bf16[128,5120]{1,0:T(8,128)(2,1)} async-done(((bf16[32,5120]{1,0:T(8,128)(2,1)}), bf16[128,5120]{1,0:T(8,128)(2,1)}) %all-gather.9.cloned.1.call-update) | async-done | bytes 1310736 | tf_op jit(solution)/shard_map/all_gather | solution.py:69
  408.8 31.5 %all_gather.43 = bf16[1024,256]{1,0:T(8,128)(2,1)S(1)} all-gather(bf16[128,256]{1,0:T(8,128)(2,1)S(1)} %get-tuple-element.26), channel_id=1, replica_groups=mesh['seq'=8,'feat'=4] {'seq'}, dimensions={0}, use_global_device_ids=true | all-gather | bytes 589824 | tf_op jit(solution)/shard_map/all_gather | solution.py:79
  442.4 33.7 %all_gather.44 = bf16[1024,256]{1,0:T(8,128)(2,1)} all-gather(bf16[128,256]{1,0:T(8,128)(2,1)} %get-tuple-element.25), channel_id=1, replica_groups=mesh['seq'=8,'feat'=4] {'seq'}, dimensions={0}, use_global_device_ids=true | all-gather | bytes 589824 | tf_op jit(solution)/shard_map/all_gather | solution.py:78
  485.9 34.5 %reduce-scatter.9.cloned.1.call-done = f32[32,5120]{1,0:T(8,128)} async-done(((f32[128,5120]{1,0:T(8,128)}), f32[32,5120]{1,0:T(8,128)}) %reduce-scatter.9.cloned.1.call-update) | async-done | bytes 655376 | tf_op jit(solution)/shard_map/reduce_scatter | solution.py:101
  525.7 13.0 %fusion.42 = f32[3,3]{1,0:T(4,128)S(1)} fusion(f32[3,32,5120]{2,1,0:T(8,128)S(1)} %pad_maximum_fusion.1), kind=kOutput, calls=%fused_computation.45 | convolution fusion | flops 17694720 | bytes 1966116 | tf_op jit(solution)/shard_map/dot_general | solution.py:118
  538.7 39.2 %psum.22 = f32[3,3]{1,0:T(4,128)S(1)} all-reduce(f32[3,3]{1,0:T(4,128)S(1)} %fusion.42), channel_id=1, replica_groups=mesh['seq'=8,'feat'=4] {'seq','feat'}, use_global_device_ids=true, to_apply=%region_16.17 | all-reduce | flops 9 | bytes 72 | tf_op jit(solution)/shard_map/psum | solution.py:119
  593.7 19.0 %all-gather.11.cloned.1.call-done = bf16[128,5120]{1,0:T(8,128)(2,1)} async-done(((bf16[32,5120]{1,0:T(8,128)(2,1)}), bf16[128,5120]{1,0:T(8,128)(2,1)}) %all-gather.11.cloned.1.call-update) | async-done | bytes 1310736 | tf_op jit(solution)/shard_map/all_gather | solution.py:69
  622.7 31.6 %all_gather.46 = bf16[1024,256]{1,0:T(8,128)(2,1)S(1)} all-gather(bf16[128,256]{1,0:T(8,128)(2,1)S(1)} %get-tuple-element.24), channel_id=1, replica_groups=mesh['seq'=8,'feat'=4] {'seq'}, dimensions={0}, use_global_device_ids=true | all-gather | bytes 589824 | tf_op jit(solution)/shard_map/all_gather | solution.py:79
  657.2 33.8 %all_gather.47 = bf16[1024,256]{1,0:T(8,128)(2,1)} all-gather(bf16[128,256]{1,0:T(8,128)(2,1)S(1)} %get-tuple-element.23), channel_id=1, replica_groups=mesh['seq'=8,'feat'=4] {'seq'}, dimensions={0}, use_global_device_ids=true | all-gather | bytes 589824 | tf_op jit(solution)/shard_map/all_gather | solution.py:78
  701.4 34.8 %reduce-scatter.11.cloned.1.call-done = f32[32,5120]{1,0:T(8,128)} async-done(((f32[128,5120]{1,0:T(8,128)}), f32[32,5120]{1,0:T(8,128)}) %reduce-scatter.11.cloned.1.call-update) | async-done | bytes 655376 | tf_op jit(solution)/shard_map/reduce_scatter | solution.py:101
  741.2 13.6 %fusion.45 = f32[4,4]{1,0:T(4,128)S(1)} fusion(f32[4,32,5120]{2,1,0:T(8,128)S(1)} %pad_maximum_fusion), kind=kOutput, calls=%fused_computation.46 | convolution fusion | flops 31457280 | bytes 2621504 | tf_op jit(solution)/shard_map/dot_general | solution.py:118
  754.9 39.2 %psum.23 = f32[4,4]{1,0:T(4,128)S(1)} all-reduce(f32[4,4]{1,0:T(4,128)S(1)} %fusion.45), channel_id=1, replica_groups=mesh['seq'=8,'feat'=4] {'seq','feat'}, use_global_device_ids=true, to_apply=%region_22.23 | all-reduce | flops 16 | bytes 128 | tf_op jit(solution)/shard_map/psum | solution.py:119
  817.3 13.6 %all_to_all.46 = f32[32,4,1280]{2,0,1:T(8,128)S(1)} all-to-all(f32[32,4,1280]{2,0,1:T(8,128)S(1)} %bitcast.240), channel_id=1, replica_groups=mesh['seq'=8,'feat'=4] {'feat'}, dimensions={1} | all-to-all | bytes 1310720 | tf_op jit(solution)/shard_map/all_to_all | solution.py:124
  (192 shorter events, 153.5 us)
Async XLA Ops:
  6.5 21.6 %copy-start.13 = (f32[5120]{0:T(1024)S(1)}, f32[5120]{0:T(1024)}, u32[]{:S(2)}) copy-start(f32[5120]{0:T(1024)} %param.10) | copy-start | bytes 61444
  17.6 10.1 %all-to-all-start = ((bf16[4,32,1280]{2,1,0:T(8,128)(2,1)}), bf16[4,32,1280]{2,1,0:T(8,128)(2,1)S(1)}, u32[]{:S(2)}, u32[]{:S(2)}) async-start(bf16[4,32,1280]{2,1,0:T(8,128)(2,1)} %bitcast.260), calls=%async_computation | async-start | bytes 655360 | tf_op jit(solution)/shard_map/all_to_all | solution.py:57
  21.1 27.2 %all-gather.5.cloned.1.call-start = ((), (), s32[]{:S(2)}) async-start(), calls=%async_computation.7 | async-start | bytes 1638400 | tf_op jit(solution)/shard_map/all_gather | solution.py:69
  29.0 142.2 %reduce-scatter.5.cloned.1.call-start = ((), (), s32[]{:S(2)}) async-start(), calls=%async_computation.8 | async-start | bytes 3276800 | tf_op jit(solution)/shard_map/reduce_scatter | solution.py:101
  39.9 3.7 copy-start.7
  90.7 41.4 %slice-start = ((s8[13107200]{0:T(1024)(128)(4,1)}), s8[524288]{0:T(1024)(128)(4,1)S(1)}, s32[]{:S(2)}) async-start(s8[13107200]{0:T(1024)(128)(4,1)} %bitcast.226), calls=%async_computation.15 | async-start | bytes 1048576
  127.2 3.4 copy-start.10
  127.2 4.8 slice-start.1
  133.0 39.5 %copy-start.8 = (f32[5120]{0:T(1024)S(1)}, f32[5120]{0:T(1024)}, u32[]{:S(2)}) copy-start(f32[5120]{0:T(1024)} %param.11) | copy-start | bytes 61444
  136.4 56.4 %all-gather.7.cloned.1.call-start = ((), (), s32[]{:S(2)}) async-start(), calls=%async_computation.9 | async-start | bytes 1638400 | tf_op jit(solution)/shard_map/all_gather | solution.py:69
  172.8 145.5 %copy-start = (f32[1,32,5120]{2,1,0:T(8,128)}, f32[1,32,5120]{2,1,0:T(8,128)S(1)}, u32[]{:S(2)}) copy-start(f32[1,32,5120]{2,1,0:T(8,128)S(1)} %get-tuple-element.22) | copy-start | bytes 1966084
  174.5 141.2 %reduce-scatter.7.cloned.1.call-start = ((), (), s32[]{:S(2)}) async-start(), calls=%async_computation.10 | async-start | bytes 3276800 | tf_op jit(solution)/shard_map/reduce_scatter | solution.py:101
  235.2 41.4 %slice-start.4 = ((s8[13107200]{0:T(1024)(128)(4,1)}), s8[524288]{0:T(1024)(128)(4,1)S(1)}, s32[]{:S(2)}) async-start(s8[13107200]{0:T(1024)(128)(4,1)} %bitcast.228), calls=%async_computation.19 | async-start | bytes 1048576
  271.8 3.4 copy-start.11
  271.8 4.8 slice-start.5
  281.0 117.3 %all-gather.9.cloned.1.call-start = ((), (), s32[]{:S(2)}) async-start(), calls=%async_computation.11 | async-start | bytes 1638400 | tf_op jit(solution)/shard_map/all_gather | solution.py:69
  379.2 141.3 %reduce-scatter.9.cloned.1.call-start = ((), (), s32[]{:S(2)}) async-start(), calls=%async_computation.12 | async-start | bytes 3276800 | tf_op jit(solution)/shard_map/reduce_scatter | solution.py:101
  440.2 40.7 %slice-start.8 = ((s8[13107200]{0:T(1024)(128)(4,1)}), s8[524288]{0:T(1024)(128)(4,1)S(1)}, s32[]{:S(2)}) async-start(s8[13107200]{0:T(1024)(128)(4,1)} %bitcast.230), calls=%async_computation.23 | async-start | bytes 1048576
  477.3 3.7 slice-start.9
  485.6 127.1 %all-gather.11.cloned.1.call-start = ((), (), s32[]{:S(2)}) async-start(), calls=%async_computation.13 | async-start | bytes 1638400 | tf_op jit(solution)/shard_map/all_gather | solution.py:69
  593.7 142.5 %reduce-scatter.11.cloned.1.call-start = ((), (), s32[]{:S(2)}) async-start(), calls=%async_computation.14 | async-start | bytes 3276800 | tf_op jit(solution)/shard_map/reduce_scatter | solution.py:101
  622.7 74.3 %slice-start.12 = ((s8[13107200]{0:T(1024)(128)(4,1)}), s8[524288]{0:T(1024)(128)(4,1)S(1)}, s32[]{:S(2)}) async-start(s8[13107200]{0:T(1024)(128)(4,1)} %bitcast.232), calls=%async_computation.27 | async-start | bytes 1048576
  692.1 4.8 slice-start.13
  701.4 38.4 %copy-start.1 = (f32[1,32,5120]{2,1,0:T(8,128)S(1)}, f32[1,32,5120]{2,1,0:T(8,128)}, u32[]{:S(2)}) copy-start(f32[1,32,5120]{2,1,0:T(8,128)} %copy-done) | copy-start | bytes 1966084
  (15 other events, 31.1 us)
Sparse Core Ops, SparseCore 0:
  29.1 19.0 all-gather.4
  136.5 34.6 reduce-scatter.4
  174.7 18.1 all-gather.6
  281.1 34.6 reduce-scatter.6
  379.3 18.8 all-gather.8
  485.8 34.6 reduce-scatter.8
  593.8 18.8 all-gather.10
  701.5 34.6 reduce-scatter.10
where the time goes:
time: 848 us; the launch traced here: 839 us
  blocking collectives  403 us (48%)
  waiting for transfers between devices  204 us (24%)
  matrix products  102 us (12%)
  local copies, waits for them, and re-layouts  54.8 us (6%)
  between operations  39 us (5%)
  other arithmetic  31.9 us (4%)
    reduce_scatter x4, waiting for transfers between devices, on_device(): lax.psum_scatter(jnp.dot(attended, w_out, preferred_element_type=jnp.floa...  138 us
    all_gather x4, blocking collectives, on_device(): key_piece = lax.all_gather(key_rows, 'seq', axis=0, tiled=True)  134 us
    all_gather x4, blocking collectives, on_device(): value_piece = lax.all_gather(value_rows, 'seq', axis=0, tiled=True)  126 us
    psum x3, blocking collectives, on_device(): gram_matrix = lax.psum(local_gram, ('seq', 'feat'))  118 us
    all_gather x4, waiting for transfers between devices, on_device(): lax.all_gather(normed, 'feat', axis=0, tiled=True)  58.7 us
    dot_general x3, matrix products, on_device(): local_gram = jnp.dot(stacked, stacked.T, precision=lax.Precision.HIGHEST)  38.6 us
    dot_general x4, matrix products, on_device(): jnp.dot(lax.all_gather(normed, 'feat', axis=0, tiled=True), w_joined, pre...  36.7 us
    unnamed x63, local copies, waits for them, and re-layouts  23.7 us
  transfers between devices with their start and end apart: 9, of which 9 were waited for; matrix products, arithmetic and copies ran while one was open for 2% of the time, Pallas kernels for 0%

commit v1 on v0

v1 whole, which is shorter than its diff:
```python
import functools
import math

import jax
import jax.numpy as jnp
from jax import lax
from jax.experimental import pallas as pl
from jax.experimental.pallas import tpu as pltpu
from jax.sharding import PartitionSpec as P

HEADS = 40
KV_HEADS = 8
HEAD_DIM = 128
ITERS = 4

EPS = 1e-06
LAMBDA = 0.03
MESH = pl.DeviceIdType.MESH
VMEM = pl.BlockSpec(memory_space=pltpu.VMEM)


def greet(axis, peers):
    barrier = pltpu.get_barrier_semaphore()
    for peer in peers:
        pl.semaphore_signal(barrier, inc=1, device_id={axis: peer}, device_id_type=MESH)
    return barrier


def send(src, dst, send_sem, recv_sem, axis, target):
    copy = pltpu.make_async_remote_copy(
        src_ref=src, dst_ref=dst, send_sem=send_sem, recv_sem=recv_sem,
        device_id={axis: target}, device_id_type=MESH,
    )
    copy.start()
    return copy


def place(axis, n):
    me = lax.axis_index(axis)
    side = lax.rem(me, 2)
    mine = lax.div(me, 2)
    return me, side, mine, me + 1 - 2 * side, n // 2


def gather_kernel(axis, n, chunks, x_ref, o_ref, send_sem, recv_sem, own_sem):
    me, side, mine, partner, lines = place(axis, n)
    rows = x_ref.shape[0] // chunks
    peers = [2 * lax.rem(mine + d, lines) + side for d in range(1, lines)]
    barrier = greet(axis, [partner] + peers)
    own = pltpu.make_async_copy(x_ref, o_ref.at[me], own_sem)
    own.start()
    pl.semaphore_wait(barrier, lines)
    pending = []
    arrivals = []
    for c in range(chunks):
        part = pl.ds(c * rows, rows)
        for d in range(1, lines):
            copy = send(x_ref.at[part], o_ref.at[me, part], send_sem.at[c, d], recv_sem.at[c, d], axis, peers[d - 1])
            arrivals.append((c, d, copy))
    for c in range(chunks):
        part = pl.ds(c * rows, rows)
        pending.append(
            send(x_ref.at[part], o_ref.at[me, part], send_sem.at[c, 0], recv_sem.at[c, 0], axis, partner)
        )
    for c, d, copy in arrivals:
        copy.wait_recv()
        part = pl.ds(c * rows, rows)
        source = 2 * lax.rem(mine - d + lines, lines) + side
        here = o_ref.at[source, part]
        at = lines - 1 + d
        pending.append(send(here, here, send_sem.at[c, at], recv_sem.at[c, at], axis, partner))
    for c, d, copy in arrivals:
        copy.wait_send()
    for copy in pending:
        copy.wait()
    own.wait()


def gather(x, axis, chunks, collective_id):
    n = lax.axis_size(axis)
    return pl.pallas_call(
        functools.partial(gather_kernel, axis, n, chunks),
        out_shape=jax.ShapeDtypeStruct((n,) + x.shape, x.dtype),
        in_specs=[VMEM],
        out_specs=VMEM,
        scratch_shapes=[
            pltpu.SemaphoreType.DMA((chunks, n)),
            pltpu.SemaphoreType.DMA((chunks, n)),
            pltpu.SemaphoreType.DMA,
        ],
        compiler_params=pltpu.CompilerParams(collective_id=collective_id, has_side_effects=True),
    )(x)


def scatter_kernel(axis, n, chunks, x_ref, o_ref, near, outgoing, far, near_s, near_r, far_s, far_r):
    me, side, mine, partner, lines = place(axis, n)
    rows = x_ref.shape[1] // chunks
    lined = [lax.rem(mine + d, lines) for d in range(lines)]
    barrier = greet(axis, [partner] + [2 * line + side for line in lined[1:]])
    pl.semaphore_wait(barrier, lines)
    nears = {}
    for c in range(chunks):
        part = pl.ds(c * rows, rows)
        for d in range(1, lines):
            nears[c, d] = send(
                x_ref.at[2 * lined[d] + 1 - side, part], near.at[d, part],
                near_s.at[c, d], near_r.at[c, d], axis, partner,
            )
    for c in range(chunks):
        part = pl.ds(c * rows, rows)
        nears[c, 0] = send(
            x_ref.at[partner, part], near.at[0, part], near_s.at[c, 0], near_r.at[c, 0], axis, partner
        )
    fars = {}
    for c in range(chunks):
        part = pl.ds(c * rows, rows)
        for d in range(1, lines):
            nears[c, d].wait_recv()
            outgoing[d, part] = (
                x_ref[2 * lined[d] + side, part].astype(jnp.float32) + near[d, part].astype(jnp.float32)
            ).astype(jnp.bfloat16)
            fars[c, d] = send(
                outgoing.at[d, part], far.at[d, part], far_s.at[c, d], far_r.at[c, d], axis,
                2 * lined[d] + side,
            )
    for c in range(chunks):
        part = pl.ds(c * rows, rows)
        nears[c, 0].wait_recv()
        total = x_ref[me, part].astype(jnp.float32) + near[0, part].astype(jnp.float32)
        for d in range(1, lines):
            fars[c, d].wait_recv()
            total = total + far[d, part].astype(jnp.float32)
        o_ref[part] = total
    for copy in list(nears.values()) + list(fars.values()):
        copy.wait_send()


def scatter(x, axis, chunks, collective_id):
    n = lax.axis_size(axis)
    lines = n // 2
    buffer = pltpu.VMEM((lines,) + x.shape[1:], x.dtype)
    return pl.pallas_call(
        functools.partial(scatter_kernel, axis, n, chunks),
        out_shape=jax.ShapeDtypeStruct(x.shape[1:], jnp.float32),
        in_specs=[VMEM],
        out_specs=VMEM,
        scratch_shapes=[buffer] * 3 + [pltpu.SemaphoreType.DMA((chunks, lines))] * 4,
        compiler_params=pltpu.CompilerParams(collective_id=collective_id, has_side_effects=True),
    )(x)


def exchange_kernel(axis, n, x_ref, o_ref, send_sem, recv_sem, own_sem):
    me = lax.axis_index(axis)
    peers = [lax.rem(me + d, n) for d in range(1, n)]
    barrier = greet(axis, peers)
    own = pltpu.make_async_copy(x_ref.at[me], o_ref.at[me], own_sem)
    own.start()
    pl.semaphore_wait(barrier, n - 1)
    copies = [
        send(x_ref.at[peer], o_ref.at[me], send_sem.at[d], recv_sem.at[d], axis, peer)
        for d, peer in enumerate(peers)
    ]
    for copy in copies:
        copy.wait()
    own.wait()


def exchange(x, axis, collective_id):
    n = lax.axis_size(axis)
    return pl.pallas_call(
        functools.partial(exchange_kernel, axis, n),
        out_shape=jax.ShapeDtypeStruct(x.shape, x.dtype),
        in_specs=[VMEM],
        out_specs=VMEM,
        scratch_shapes=[
            pltpu.SemaphoreType.DMA((n,)),
            pltpu.SemaphoreType.DMA((n,)),
            pltpu.SemaphoreType.DMA,
        ],
        compiler_params=pltpu.CompilerParams(collective_id=collective_id, has_side_effects=True),
    )(x)


def solve_values(rows, values):
    size = len(values)
    rows = [list(row) for row in rows]
    values = list(values)
    for pivot in range(size):
        for below in range(pivot + 1, size):
            ratio = rows[below][pivot] / rows[pivot][pivot]
            for at in range(pivot, size):
                rows[below][at] = rows[below][at] - ratio * rows[pivot][at]
            values[below] = values[below] - ratio * values[pivot]
    result = [None] * size
    for pivot in reversed(range(size)):
        running = values[pivot]
        for later in range(pivot + 1, size):
            running = running - rows[pivot][later] * result[later]
        result[pivot] = running / rows[pivot][pivot]
    return result


def new_products(count):
    return [(i, j) for i in range(count) for j in range(i + 1) if i == count - 1 or count == 2]


def mix_kernel(axes, sizes, count, scale_all, *refs):
    images = refs[:count]
    residuals = refs[count : 2 * count]
    prior = refs[2 * count]
    o_ref, gram_ref, out_ref, slots0, slots1, held0, held1, s0, r0, s1, r1 = refs[2 * count + 1 :]
    slots, held, send_sems, recv_sems = (slots0, slots1), (held0, held1), (s0, s1), (r0, r1)
    barrier = pltpu.get_barrier_semaphore()
    peers = []
    for axis, n in zip(axes, sizes):
        me = lax.axis_index(axis)
        peers.append([lax.rem(me + d, n) for d in range(1, n)])
        for peer in peers[-1]:
            pl.semaphore_signal(barrier, inc=1, device_id={axis: peer}, device_id_type=MESH)
    rows, width = images[0].shape
    wanted = new_products(count)

    def block(at, sums):
        columns = pl.ds(pl.multiple_of(at * 128, 128), 128)
        return tuple(
            total + jnp.sum((residuals[i][:, columns] * residuals[j][:, columns]).reshape(rows // 8, 8, 128), axis=0)
            for (i, j), total in zip(wanted, sums)
        )

    zero = jnp.zeros((8, 128), jnp.float32)
    sums = lax.fori_loop(0, width // 128, block, (zero,) * len(wanted), unroll=4)
    pl.semaphore_wait(barrier, sum(sizes) - len(sizes))
    local = jnp.concatenate(sums, axis=0)
    for stage, axis in enumerate(axes):
        held[stage][...] = local
        copies = [
            send(held[stage], slots[stage].at[d], send_sems[stage].at[d], recv_sems[stage].at[d], axis, peer)
            for d, peer in enumerate(peers[stage])
        ]
        for d, copy in enumerate(copies):
            copy.wait()
            local = local + slots[stage][d]
    gram = [[None] * count for _ in range(count)]
    for i in range(count):
        for j in range(i + 1):
            if (i, j) in wanted:
                at = 8 * wanted.index((i, j))
                value = jnp.broadcast_to(jnp.sum(local[at : at + 8], keepdims=True), (8, 128))
            else:
                value = prior[ITERS * i + j]
            gram[i][j] = gram[j][i] = value
    for i in range(ITERS):
        for j in range(ITERS):
            if i < count and j <= i:
                gram_ref[ITERS * i + j] = gram[i][j]
            else:
                gram_ref[ITERS * i + j] = zero
    system = [
        [gram[i][j] / scale_all + (LAMBDA if i == j else 0.0) for j in range(count)] for i in range(count)
    ]
    unscaled = solve_values(system, [jnp.ones((8, 128), jnp.float32)] * count)
    whole = unscaled[0]
    for value in unscaled[1:]:
        whole = whole + value
    weights = [value / whole for value in unscaled]
    for j in range(count):
        out_ref[j] = weights[j]
    tiles = [jnp.broadcast_to(weight[:1], (rows, 128)) for weight in weights]

    def combine(at, carry):
        columns = pl.ds(pl.multiple_of(at * 128, 128), 128)
        total = tiles[0] * images[0][:, columns]
        for j in range(1, count):
            total = total + tiles[j] * images[j][:, columns]
        o_ref[:, columns] = total
        return carry

    lax.fori_loop(0, width // 128, combine, 0, unroll=4)


def mix(images, residuals, prior, axes, scale_all, collective_id):
    sizes = tuple(lax.axis_size(axis) for axis in axes)
    count = len(images)
    current, gram, _ = pl.pallas_call(
        functools.partial(mix_kernel, axes, sizes, count, scale_all),
        out_shape=[
            jax.ShapeDtypeStruct(images[0].shape, jnp.float32),
            jax.ShapeDtypeStruct((ITERS * ITERS, 8, 128), jnp.float32),
            jax.ShapeDtypeStruct((count, 8, 128), jnp.float32),
        ],
        in_specs=[VMEM] * (2 * count + 1),
        out_specs=[VMEM] * 3,
        scratch_shapes=[pltpu.VMEM((n, 8 * len(new_products(count)), 128), jnp.float32) for n in sizes]
        + [pltpu.VMEM((8 * len(new_products(count)), 128), jnp.float32)] * len(sizes)
        + [pltpu.SemaphoreType.DMA((n,)) for n in sizes for _ in range(2)],
        compiler_params=pltpu.CompilerParams(collective_id=collective_id, has_side_effects=True),
    )(*images, *residuals, prior)
    return current, gram


def on_device(injection, warm_start, gain_in, gain_out, w_query, w_key, w_value, w_out):
    seq_at = lax.axis_index("seq")
    feat = lax.axis_size("feat")
    seq = lax.axis_size("seq")
    tok_dev = injection.shape[0]
    width = gain_in.shape[0]
    head_cols = w_query.shape[1]
    kv_cols = w_key.shape[1]
    kv_local = kv_cols // HEAD_DIM
    group = HEADS // KV_HEADS
    rows = tok_dev // feat
    part = width // feat
    scale_all = float(tok_dev * seq * width)
    score_scale = 1.0 / math.sqrt(HEAD_DIM)
    w_kv = jnp.concatenate([w_key, w_value], axis=1)
    query_pos = seq_at * tok_dev + jnp.arange(tok_dev, dtype=jnp.int32)
    key_pos = jnp.arange(tok_dev * seq, dtype=jnp.int32)
    allowed = (query_pos[:, None] >= key_pos[None, :])[:, None, :]
    start = jnp.stack([injection.reshape(feat, rows, part), warm_start.reshape(feat, rows, part)], axis=1)
    start = exchange(start, "feat", 0).transpose(1, 2, 0, 3).reshape(2, rows, width).astype(jnp.float32)
    injection_full, current = start[0], start[1]
    evaluated = []
    residuals = []
    gram = None
    for iteration in range(ITERS):
        mixed = current + injection_full
        normed = (
            mixed * lax.rsqrt(jnp.mean(mixed * mixed, axis=1, keepdims=True) + EPS) * gain_in
        ).astype(jnp.bfloat16)
        tokens = gather(normed, "feat", 2, 1).reshape(tok_dev, width)
        key_value = jnp.dot(tokens, w_kv, preferred_element_type=jnp.float32).astype(jnp.bfloat16)
        queries = jnp.dot(tokens, w_query, preferred_element_type=jnp.float32).astype(jnp.bfloat16)
        pieces = gather(key_value, "seq", 1, 2).reshape(seq * tok_dev, 2 * kv_cols)
        heads = []
        for e in range(kv_local):
            key_head = pieces[:, e * HEAD_DIM : (e + 1) * HEAD_DIM]
            value_head = pieces[:, kv_cols + e * HEAD_DIM : kv_cols + (e + 1) * HEAD_DIM]
            query_head = queries[:, e * group * HEAD_DIM : (e + 1) * group * HEAD_DIM].reshape(
                tok_dev, group, HEAD_DIM
            )
            scores = (
                jnp.einsum("tgd,sd->tgs", query_head, key_head, preferred_element_type=jnp.float32)
                * score_scale
            )
            scores = jnp.where(allowed, scores, -1e30)
            weights = jnp.where(allowed, jnp.exp(scores - jnp.max(scores, axis=2, keepdims=True)), 0.0)
            row_sum = jnp.sum(weights, axis=2, keepdims=True)
            summed = jnp.einsum(
                "tgs,sd->tgd", weights.astype(jnp.bfloat16), value_head, preferred_element_type=jnp.float32
            )
            heads.append((summed / row_sum).astype(jnp.bfloat16).reshape(tok_dev, group * HEAD_DIM))
        attended = jnp.concatenate(heads, axis=1)
        partial = jnp.dot(attended, w_out, preferred_element_type=jnp.float32).astype(jnp.bfloat16)
        update = scatter(partial.reshape(feat, rows, width), "feat", 2, 3)
        summed = mixed + update
        image = (
            summed * lax.rsqrt(jnp.mean(summed * summed, axis=1, keepdims=True) + EPS) * gain_out
        )
        evaluated.append(image)
        residuals.append(image - current)
        if iteration == 0:
            current = image
            gram = jnp.zeros((ITERS * ITERS, 8, 128), jnp.float32)
        else:
            current, gram = mix(evaluated, residuals, gram, ("feat", "seq"), scale_all, 4 + iteration)
    final = current.reshape(rows, feat, part).transpose(1, 0, 2)
    return exchange(final, "feat", 4).reshape(tok_dev, part)


def solution(mesh):
    in_specs = (
        P("seq", "feat"),
        P("seq", "feat"),
        P(),
        P(),
        P(None, "feat"),
        P(None, "feat"),
        P(None, "feat"),
        P("feat", None),
    )
    out_specs = P("seq", "feat")
    return jax.shard_map(
        on_device, mesh=mesh, in_specs=in_specs, out_specs=out_specs, check_vma=False
    )
```

time: 848 us -> 411 us (0.48)
  blocking collectives: 403 us -> 0 us
  Pallas kernels: 0 us -> 265 us
  waiting for transfers between devices: 204 us -> 0 us
  local copies, waits for them, and re-layouts: 54.8 us -> 14.2 us
  between operations: 39 us -> 0.97 us
  other arithmetic: 31.9 us -> 20.3 us
    pallas_call x0 -> x17, Pallas kernels: none -> 265 us  [the longest x8 144 us: gather(): pl.pallas_call(functools.partial(gather_kernel, axis, n, chunks), out_sha...]
    all_gather x8 -> x0, blocking collectives: 260 us -> none  [the longest x4 134 us: on_device(): key_piece = lax.all_gather(key_rows, 'seq', axis=0, tiled=True)]
    reduce_scatter x4 -> x0, waiting for transfers between devices: 138 us -> none  [on_device(): lax.psum_scatter(jnp.dot(attended, w_out, preferred_element_type=jnp.floa...]
    psum x3 -> x0, blocking collectives: 118 us -> none  [on_device(): gram_matrix = lax.psum(local_gram, ('seq', 'feat'))]
    all_gather x4 -> x0, waiting for transfers between devices: 58.7 us -> none  [on_device(): lax.all_gather(normed, 'feat', axis=0, tiled=True)]
    dot_general x15 -> x16, matrix products: 88.2 us -> 57 us  [the longest x4 26.4 us: on_device(): jnp.dot(tokens, w_query, preferred_element_type=jnp.float32)]
    all_to_all x2 -> x0, blocking collectives: 24.7 us -> none  [the longest x1 13.6 us: on_device(): lax.all_to_all(current, 'feat', split_axis=1, concat_axis=0, tiled=True)]
    dot_general x4, matrix products: 13.6 us -> 31 us  [on_device(): jnp.dot(attended, w_out, preferred_element_type=jnp.float32)]
  transfers between devices with their start and end apart: 9 -> 0, of which waited for: 9 -> 0; matrix products, arithmetic and copies ran while one was open for 2% -> 0% of each run, Pallas kernels for 0% -> 0%
where the time goes in v1:
time: 411 us; the launch traced here: 405 us
  Pallas kernels  265 us (64%)
  matrix products  105 us (26%)
  other arithmetic  20.3 us (5%)
  local copies, waits for them, and re-layouts  14.2 us (3%)
    pallas_call x8, Pallas kernels, gather(): pl.pallas_call(functools.partial(gather_kernel, axis, n, chunks), out_sha...  144 us
    pallas_call x4, Pallas kernels, scatter(): pl.pallas_call(functools.partial(scatter_kernel, axis, n, chunks), out_sh...  50.7 us
    pallas_call x3, Pallas kernels, mix(): pl.pallas_call(functools.partial(mix_kernel, axes, sizes, count, scale_al...  47.4 us
    dot_general x4, matrix products, on_device(): jnp.dot(attended, w_out, preferred_element_type=jnp.float32)  31 us
    dot_general x4, matrix products, on_device(): jnp.dot(tokens, w_query, preferred_element_type=jnp.float32)  26.4 us
    pallas_call x2, Pallas kernels, exchange(): pl.pallas_call(functools.partial(exchange_kernel, axis, n), out_shape=jax...  22.5 us
    sub x8, matrix products, on_device(): scores - jnp.max(scores, axis=2, keepdims=True)  17.1 us
    dot_general x8, matrix products, on_device(): jnp.einsum('tgs,sd->tgd', weights.astype(jnp.bfloat16), value_head, prefe...  15.5 us

profile of v1, /device:TPU:0, one launch (start us, length us, event | category | flops | bytes accessed | tf_op | source)
XLA Modules:
  0.0 405.3 jit_solution(15328856092376571746)
XLA Ops:
  2.0 12.5 %shard_map.82 = bf16[4,2,32,1280]{3,2,1,0:T(8,128)(2,1)} custom-call(bf16[4,2,32,1280]{3,2,1,0:T(8,128)(2,1)} %pad_maximum_fusion.x_ref), custom_call_target="tpu_custom_call" | custom-call | tf_op jit(solution)/shard_map/pallas_call | solution.py:170
  18.0 13.5 %shard_map.83 = bf16[4,32,5120]{2,1,0:T(8,128)(2,1)} custom-call(bf16[32,5120]{1,0:T(8,128)(2,1)} %multiply_convert_fusion.3.x_ref), custom_call_target="tpu_custom_call" | custom-call | tf_op jit(solution)/shard_map/pallas_call | solution.py:81
  38.2 23.4 %shard_map.84 = bf16[8,128,512]{2,1,0:T(8,128)(2,1)} custom-call(bf16[128,512]{1,0:T(8,128)(2,1)} %convolution_convert_fusion.11.x_ref), custom_call_target="tpu_custom_call" | custom-call | tf_op jit(solution)/shard_map/pallas_call | solution.py:81
  79.8 7.8 %convolution_convert_fusion.3 = bf16[128,5120]{1,0:T(8,128)(2,1)} fusion(bf16[1280,5120]{1,0:T(8,128)(2,1)} %param.15, bf16[128,640]{0,1:T(8,128)(2,1)S(1)} %bitcast.248, bf16[128,640]{0,1:T(8,128)(2,1)S(1)} %bitcast.244), kind=kOutput, calls=%fused_computation.11 | convolution fusion | flops 1679032320 | bytes 14745600 | tf_op jit(solution)/shard_map/dot_general | solution.py:353
  87.6 12.3 %shard_map.85 = f32[32,5120]{1,0:T(8,128)} custom-call(bf16[4,32,5120]{2,1,0:T(8,128)(2,1)} %bitcast.216), custom_call_target="tpu_custom_call" | custom-call | tf_op jit(solution)/shard_map/pallas_call | solution.py:142
  103.2 13.5 %shard_map.86 = bf16[4,32,5120]{2,1,0:T(8,128)(2,1)} custom-call(bf16[32,5120]{1,0:T(8,128)(2,1)} %multiply_convert_fusion.2.x_ref), custom_call_target="tpu_custom_call" | custom-call | tf_op jit(solution)/shard_map/pallas_call | solution.py:81
  121.2 23.4 %shard_map.87 = bf16[8,128,512]{2,1,0:T(8,128)(2,1)} custom-call(bf16[128,512]{1,0:T(8,128)(2,1)} %convolution_convert_fusion.10.x_ref), custom_call_target="tpu_custom_call" | custom-call | tf_op jit(solution)/shard_map/pallas_call | solution.py:81
  144.6 6.6 %convolution_convert_fusion.6 = bf16[128,1280]{1,0:T(8,128)(2,1)S(1)} fusion(bf16[128,5120]{1,0:T(8,128)(2,1)S(1)} %bitcast.211, bf16[5120,1280]{1,0:T(8,128)(2,1)} %param.12), kind=kOutput, calls=%fused_computation.30 | convolution fusion | flops 1677885440 | bytes 14745600 | tf_op jit(solution)/shard_map/dot_general | solution.py:332
  162.7 7.8 %convolution_convert_fusion.2 = bf16[128,5120]{1,0:T(8,128)(2,1)} fusion(bf16[1280,5120]{1,0:T(8,128)(2,1)} %param.15, bf16[128,640]{0,1:T(8,128)(2,1)S(1)} %bitcast.249, bf16[128,640]{0,1:T(8,128)(2,1)S(1)} %bitcast.245), kind=kOutput, calls=%fused_computation.10 | convolution fusion | flops 1679032320 | bytes 14745600 | tf_op jit(solution)/shard_map/dot_general | solution.py:353
  170.5 12.4 %shard_map.88 = f32[32,5120]{1,0:T(8,128)} custom-call(bf16[4,32,5120]{2,1,0:T(8,128)(2,1)} %bitcast.217), custom_call_target="tpu_custom_call" | custom-call | tf_op jit(solution)/shard_map/pallas_call | solution.py:142
  186.1 15.7 %shard_map.89 = (f32[32,5120]{1,0:T(8,128)}, f32[16,8,128]{2,1,0:T(8,128)}, f32[2,8,128]{2,1,0:T(8,128)}) custom-call(f32[32,5120]{1,0:T(8,128)} %copy-done.1, f32[32,5120]{1,0:T(8,128)} %get-tuple-element.28.refs_1_, f32[32,5120]{1,0:T(8,128)} %get-tuple-element.29.refs_2_.refs_3_.refs_4_, f32[32,5120]{1,0:T(8,128)} %get-tuple-element.27.refs_3_.refs_4_.refs_5_, ...), custom_call_target="tpu_custom_call" | custom-call | tf_op jit(solution)/shard_map/pallas_call | solution.py:284
  203.9 12.6 %shard_map.90 = bf16[4,32,5120]{2,1,0:T(8,128)(2,1)} custom-call(bf16[32,5120]{1,0:T(8,128)(2,1)} %multiply_convert_fusion.1.x_ref), custom_call_target="tpu_custom_call" | custom-call | tf_op jit(solution)/shard_map/pallas_call | solution.py:81
  221.0 22.4 %shard_map.91 = bf16[8,128,512]{2,1,0:T(8,128)(2,1)} custom-call(bf16[128,512]{1,0:T(8,128)(2,1)} %convolution_convert_fusion.9.x_ref), custom_call_target="tpu_custom_call" | custom-call | tf_op jit(solution)/shard_map/pallas_call | solution.py:81
  243.5 6.6 %convolution_convert_fusion.5 = bf16[128,1280]{1,0:T(8,128)(2,1)S(1)} fusion(bf16[128,5120]{1,0:T(8,128)(2,1)S(1)} %bitcast.213, bf16[5120,1280]{1,0:T(8,128)(2,1)} %param.12), kind=kOutput, calls=%fused_computation.29 | convolution fusion | flops 1677885440 | bytes 14745600 | tf_op jit(solution)/shard_map/dot_general | solution.py:332
  257.1 7.7 %convolution_convert_fusion.1 = bf16[128,5120]{1,0:T(8,128)(2,1)} fusion(bf16[1280,5120]{1,0:T(8,128)(2,1)} %param.15, bf16[128,640]{0,1:T(8,128)(2,1)S(1)} %bitcast.250, bf16[128,640]{0,1:T(8,128)(2,1)S(1)} %bitcast.246), kind=kOutput, calls=%fused_computation.9 | convolution fusion | flops 1679032320 | bytes 14745600 | tf_op jit(solution)/shard_map/dot_general | solution.py:353
  264.9 13.7 %shard_map.92 = f32[32,5120]{1,0:T(8,128)} custom-call(bf16[4,32,5120]{2,1,0:T(8,128)(2,1)} %bitcast.218), custom_call_target="tpu_custom_call" | custom-call | tf_op jit(solution)/shard_map/pallas_call | solution.py:142
  281.1 14.6 %shard_map.93 = (f32[32,5120]{1,0:T(8,128)}, f32[16,8,128]{2,1,0:T(8,128)}, f32[3,8,128]{2,1,0:T(8,128)}) custom-call(f32[32,5120]{1,0:T(8,128)} %copy-done.1, f32[32,5120]{1,0:T(8,128)} %get-tuple-element.28.refs_1_, f32[32,5120]{1,0:T(8,128)} %get-tuple-element.22.refs_2_, f32[32,5120]{1,0:T(8,128)} %get-tuple-element.29.refs_2_.refs_3_.refs_4_, ...), custom_call_target="tpu_custom_call" | custom-call | tf_op jit(solution)/shard_map/pallas_call | solution.py:284
  297.9 13.3 %shard_map.94 = bf16[4,32,5120]{2,1,0:T(8,128)(2,1)} custom-call(bf16[32,5120]{1,0:T(8,128)(2,1)} %multiply_convert_fusion.x_ref), custom_call_target="tpu_custom_call" | custom-call | tf_op jit(solution)/shard_map/pallas_call | solution.py:81
  315.7 22.0 %shard_map.95 = bf16[8,128,512]{2,1,0:T(8,128)(2,1)} custom-call(bf16[128,512]{1,0:T(8,128)(2,1)} %convolution_convert_fusion.8.x_ref), custom_call_target="tpu_custom_call" | custom-call | tf_op jit(solution)/shard_map/pallas_call | solution.py:81
  337.7 6.6 %convolution_convert_fusion.4 = bf16[128,1280]{1,0:T(8,128)(2,1)S(1)} fusion(bf16[128,5120]{1,0:T(8,128)(2,1)S(1)} %bitcast.209, bf16[5120,1280]{1,0:T(8,128)(2,1)} %param.12), kind=kOutput, calls=%fused_computation.28 | convolution fusion | flops 1677885440 | bytes 14745600 | tf_op jit(solution)/shard_map/dot_general | solution.py:332
  351.3 7.7 %convolution_convert_fusion = bf16[128,5120]{1,0:T(8,128)(2,1)} fusion(bf16[1280,5120]{1,0:T(8,128)(2,1)} %param.15, bf16[128,640]{0,1:T(8,128)(2,1)S(1)} %bitcast.247, bf16[128,640]{0,1:T(8,128)(2,1)S(1)} %bitcast.243), kind=kOutput, calls=%fused_computation.8 | convolution fusion | flops 1679032320 | bytes 14745600 | tf_op jit(solution)/shard_map/dot_general | solution.py:353
  359.0 12.3 %shard_map.96 = f32[32,5120]{1,0:T(8,128)} custom-call(bf16[4,32,5120]{2,1,0:T(8,128)(2,1)} %bitcast.219), custom_call_target="tpu_custom_call" | custom-call | tf_op jit(solution)/shard_map/pallas_call | solution.py:142
  373.8 17.1 %shard_map.97 = (f32[32,5120]{1,0:T(8,128)}, f32[16,8,128]{2,1,0:T(8,128)}, f32[4,8,128]{2,1,0:T(8,128)}) custom-call(f32[32,5120]{1,0:T(8,128)} %copy-done.1, f32[32,5120]{1,0:T(8,128)} %get-tuple-element.28.refs_1_, f32[32,5120]{1,0:T(8,128)} %get-tuple-element.22.refs_2_, f32[32,5120]{1,0:T(8,128)} %get-tuple-element.16.refs_3_, ...), custom_call_target="tpu_custom_call" | custom-call | tf_op jit(solution)/shard_map/pallas_call | solution.py:284
  392.9 9.9 %shard_map.98 = f32[4,32,1280]{2,1,0:T(8,128)} custom-call(f32[4,32,1280]{2,1,0:T(8,128)} %bitcast.222), custom_call_target="tpu_custom_call" | custom-call | tf_op jit(solution)/shard_map/pallas_call | solution.py:170
  (107 shorter events, 88.8 us)
Async XLA Ops:
  16.4 0.8 copy-start.14
  31.6 2.5 copy-start.6
  34.1 2.5 copy-start.2
  34.3 2.3 copy-start
  68.4 0.8 copy-start.15
  69.2 2.5 copy-start.9
  87.6 13.6 %copy-start.13 = (f32[5120]{0:T(1024)S(1)}, f32[5120]{0:T(1024)}, u32[]{:S(2)}) copy-start(f32[5120]{0:T(1024)} %param.11) | copy-start | bytes 61444
  102.2 82.0 %copy-start.1 = (f32[32,5120]{1,0:T(8,128)}, f32[32,5120]{1,0:T(8,128)S(1)}, u32[]{:S(2)}) copy-start(f32[32,5120]{1,0:T(8,128)S(1)} %get-tuple-element.30.refs_0_) | copy-start | bytes 1966084
  116.7 27.9 %copy-start.4 = (bf16[4,32,5120]{2,1,0:T(8,128)(2,1)S(1)}, bf16[4,32,5120]{2,1,0:T(8,128)(2,1)}, u32[]{:S(2)}) copy-start(bf16[4,32,5120]{2,1,0:T(8,128)(2,1)} %shard_map.86) | copy-start | bytes 3932164
  151.5 0.7 copy-start.16
  152.1 2.5 copy-start.11
  216.5 27.0 %copy-start.5 = (bf16[4,32,5120]{2,1,0:T(8,128)(2,1)S(1)}, bf16[4,32,5120]{2,1,0:T(8,128)(2,1)}, u32[]{:S(2)}) copy-start(bf16[4,32,5120]{2,1,0:T(8,128)(2,1)} %shard_map.90) | copy-start | bytes 3932164
  243.5 6.9 %copy-start.17 = (pred[128,1024]{1,0:T(8,128)(4,1)S(1)}, pred[128,1024]{1,0:T(8,128)(4,1)}, u32[]{:S(2)}) copy-start(pred[128,1024]{1,0:T(8,128)(4,1)} %iota_compare_fusion) | copy-start | bytes 393220
  250.4 2.4 copy-start.12
  264.9 15.0 %copy-start.8 = (f32[32,5120]{1,0:T(8,128)S(1)}, f32[32,5120]{1,0:T(8,128)}, u32[]{:S(2)}) copy-start(f32[32,5120]{1,0:T(8,128)} %get-tuple-element.10) | copy-start | bytes 1966084
  311.2 26.5 %copy-start.3 = (bf16[4,32,5120]{2,1,0:T(8,128)(2,1)S(1)}, bf16[4,32,5120]{2,1,0:T(8,128)(2,1)}, u32[]{:S(2)}) copy-start(bf16[4,32,5120]{2,1,0:T(8,128)(2,1)} %shard_map.94) | copy-start | bytes 3932164
  344.5 2.4 copy-start.10
  359.0 13.6 %copy-start.7 = (f32[32,5120]{1,0:T(8,128)S(1)}, f32[32,5120]{1,0:T(8,128)}, u32[]{:S(2)}) copy-start(f32[32,5120]{1,0:T(8,128)} %get-tuple-element.12) | copy-start | bytes 1966084
